TPU v7x, 32 devices: a whole 2x2x4 slice. The times are simulated.
32 devices in a mesh: gx: 4 (over y, core), gy: 2 (over x), gz: 4 (over z).
Axes of the slice: x: 2, y: 2, z: 4, core: 2. Of those that a mesh axis runs over, the one named last changes fastest.
Arguments:
- density: float32 [32, 32, 512], P('gx', 'gy', 'gz'), may hold values from 0.7 to 1.6
- momentum: float32 [32, 32, 512], P('gx', 'gy', 'gz'), may hold values from -7 to 7
- hydrogen: float32 [32, 32, 512], P('gx', 'gy', 'gz'), may hold values from 0.05 to 1.2
- forced_modes: int32 [96, 3], replicated, may hold values from -3 to 3, as said below
Outputs:
- density_rate: float32 [32, 32, 512], P('gx', 'gy', 'gz')
- momentum_rate: float32 [32, 32, 512], P('gx', 'gy', 'gz')
- hydrogen_rate: float32 [32, 32, 512], P('gx', 'gy', 'gz')
Inputs may be any that keep to these rules, and one draw needn't show every extreme that they name: `forced_modes`: each row is a wave vector (kx, ky, kz) with 1 <= kx^2 + ky^2 + kz^2 <= 9; the 96 rows are distinct.
All inputs are finite; a program needn't handle non-finite values.
Results may differ from a plain program's by a relative error of at most 0.0003.
Values sent between devices are 32-bit elements; how exact they have to be, the bound alone decides.
A program may use at most 64 MiB of HBM per device.

v0:
```python
import jax
import jax.numpy as jnp
from jax import lax
from jax.sharding import PartitionSpec as P

KMAX = 3


FIRST_COEFFS = (0.8, -0.2, 4.0 / 105.0, -1.0 / 280.0)
SECOND_COEFFS = (1.6, -0.2, 8.0 / 315.0, -1.0 / 560.0)
CENTRE_COEFF = -205.0 / 72.0
VISCOSITY = 0.3
DIFFUSIVITY = 1.5
FORCE_POWER = 0.3
ENERGY_EPS = 1e-06
ACTIVATION = 2.0
HIGHEST = lax.Precision.HIGHEST


def padded_2(x, sides, width):
    for axis, dim in sides:
        size, length = (lax.axis_size(axis), x.shape[dim])
        up = [(i, (i + 1) % size) for i in range(size)]
        down = [(j, i) for i, j in up]
        last = lax.slice_in_dim(x, length - width, length, axis=dim)
        first = lax.slice_in_dim(x, 0, width, axis=dim)
        before = lax.ppermute(last, axis, up)
        after = lax.ppermute(first, axis, down)
        x = jnp.concatenate([before, x, after], axis=dim)
    return x


def shifted(padded, axis, offset, length):
    return lax.slice_in_dim(padded, 4 + offset, 4 + offset + length, axis=axis)


def first_diff(padded, axis, length):
    total = jnp.zeros_like(shifted(padded, axis, 0, length))
    for offset, weight in enumerate(FIRST_COEFFS, 1):
        total = total + weight * (
            shifted(padded, axis, offset, length) - shifted(padded, axis, -offset, length)
        )
    return total


def second_diff(padded, axis, length):
    total = CENTRE_COEFF * shifted(padded, axis, 0, length)
    for offset, weight in enumerate(SECOND_COEFFS, 1):
        total = total + weight * (
            shifted(padded, axis, offset, length) + shifted(padded, axis, -offset, length)
        )
    return total


def wave_tables(start, local, total):
    position = start + jnp.arange(local, dtype=jnp.int32)
    wavenum = jnp.arange(-KMAX, KMAX + 1, dtype=jnp.int32)
    phase = wavenum[:, None] * position[None, :] % total
    angle = 2.0 * jnp.pi / total * phase.astype(jnp.float32)
    return (jnp.cos(angle), jnp.sin(angle))


def modal_force(velocity, forced_modes):
    size_x, size_y, size_z = velocity.shape
    full_x = size_x * lax.axis_size("gx")
    full_y = size_y * lax.axis_size("gy")
    full_z = size_z * lax.axis_size("gz")
    cos_x, sin_x = wave_tables(lax.axis_index("gx") * size_x, size_x, full_x)
    cos_y, sin_y = wave_tables(lax.axis_index("gy") * size_y, size_y, full_y)
    cos_z, sin_z = wave_tables(lax.axis_index("gz") * size_z, size_z, full_z)
    flat = velocity.reshape(size_x * size_y, size_z)
    contract = (((1,), (1,)), ((), ()))
    part_re = lax.dot_general(cos_z, flat, contract, precision=HIGHEST).reshape(-1, size_x, size_y)
    part_im = lax.dot_general(sin_z, flat, contract, precision=HIGHEST).reshape(-1, size_x, size_y)
    mid_re = jnp.einsum("axy,by->abx", part_re, cos_y, precision=HIGHEST) - jnp.einsum(
        "axy,by->abx", part_im, sin_y, precision=HIGHEST
    )
    mid_im = jnp.einsum("axy,by->abx", part_re, sin_y, precision=HIGHEST) + jnp.einsum(
        "axy,by->abx", part_im, cos_y, precision=HIGHEST
    )
    cube_re = jnp.einsum("abx,cx->cba", mid_re, cos_x, precision=HIGHEST) - jnp.einsum(
        "abx,cx->cba", mid_im, sin_x, precision=HIGHEST
    )
    cube_im = jnp.einsum("abx,cx->cba", mid_re, sin_x, precision=HIGHEST) + jnp.einsum(
        "abx,cx->cba", mid_im, cos_x, precision=HIGHEST
    )
    width = 2 * KMAX + 1
    code = (
        (forced_modes[:, 0] + KMAX) * width * width
        + (forced_modes[:, 1] + KMAX) * width
        + (forced_modes[:, 2] + KMAX)
    )
    selector = (code[:, None] == jnp.arange(width**3, dtype=jnp.int32)[None, :]).astype(jnp.float32)
    local_cos = jnp.dot(selector, cube_re.reshape(-1), precision=HIGHEST)
    local_sin = jnp.dot(selector, cube_im.reshape(-1), precision=HIGHEST)
    summed = lax.psum((local_cos, local_sin), ("gx", "gy", "gz"))
    ncell = float(full_x * full_y * full_z)
    coef_cos = summed[0] / ncell
    coef_sin = summed[1] / ncell
    energy = jnp.sum(coef_cos * coef_cos + coef_sin * coef_sin)
    spec_re = jnp.dot(selector.T, coef_cos, precision=HIGHEST).reshape(width, width, width)
    spec_im = -jnp.dot(selector.T, coef_sin, precision=HIGHEST).reshape(width, width, width)
    step_re = jnp.einsum("abc,ax->xbc", spec_re, cos_x, precision=HIGHEST) - jnp.einsum(
        "abc,ax->xbc", spec_im, sin_x, precision=HIGHEST
    )
    step_im = jnp.einsum("abc,ax->xbc", spec_re, sin_x, precision=HIGHEST) + jnp.einsum(
        "abc,ax->xbc", spec_im, cos_x, precision=HIGHEST
    )
    plane_re = jnp.einsum("xbc,by->xyc", step_re, cos_y, precision=HIGHEST) - jnp.einsum(
        "xbc,by->xyc", step_im, sin_y, precision=HIGHEST
    )
    plane_im = jnp.einsum("xbc,by->xyc", step_re, sin_y, precision=HIGHEST) + jnp.einsum(
        "xbc,by->xyc", step_im, cos_y, precision=HIGHEST
    )
    low = 2.0 * (
        jnp.dot(plane_re.reshape(-1, width), cos_z, precision=HIGHEST)
        - jnp.dot(plane_im.reshape(-1, width), sin_z, precision=HIGHEST)
    )
    return FORCE_POWER * low.reshape(size_x, size_y, size_z) / (energy + ENERGY_EPS)


def stencil_terms(density, momentum, hydrogen):
    size_x, size_y, size_z = density.shape
    fields = jnp.stack([density, momentum, hydrogen])
    stream_pad = padded_2(fields, (("gx", 1),), 4)
    dens_pad = stream_pad[0]
    mom_pad = stream_pad[1]
    fuel_pad = stream_pad[2]
    vel_pad = mom_pad / dens_pad
    velocity = momentum / density
    mass_div = first_diff(mom_pad, 0, size_x)
    mom_div = first_diff(mom_pad * vel_pad + dens_pad, 0, size_x)
    fuel_div = first_diff(fuel_pad * vel_pad, 0, size_x)
    diffused = second_diff(stream_pad[1:], 1, size_x)
    carried = fields[1:]
    side_pad = padded_2(carried, (("gy", 2),), 4)
    diffused = diffused + second_diff(side_pad, 2, size_y)
    depth_pad = padded_2(carried, (("gz", 3),), 4)
    diffused = diffused + second_diff(depth_pad, 3, size_z)
    density_rate = -mass_div
    momentum_part = -mom_div + VISCOSITY * diffused[0]
    hydrogen_rate = (
        -fuel_div + DIFFUSIVITY * diffused[1] - hydrogen * jnp.exp(-ACTIVATION * hydrogen / density)
    )
    return (density_rate, momentum_part, hydrogen_rate, velocity)


def per_device(density, momentum, hydrogen, forced_modes):
    density_rate, momentum_part, hydrogen_rate, velocity = stencil_terms(
        density, momentum, hydrogen
    )
    force = modal_force(velocity, forced_modes)
    momentum_rate = momentum_part + density * force
    return (density_rate, momentum_rate, hydrogen_rate)


def solution(mesh):
    in_specs = (P("gx", "gy", "gz"), P("gx", "gy", "gz"), P("gx", "gy", "gz"), P())
    out_specs = (P("gx", "gy", "gz"), P("gx", "gy", "gz"), P("gx", "gy", "gz"))
    return jax.shard_map(
        per_device, mesh=mesh, in_specs=in_specs, out_specs=out_specs, check_vma=False
    )
```

profile of v0, /device:TPU:0, one launch (start us, length us, event | category | flops | bytes accessed | tf_op | source)
XLA Modules:
  0.0 68.3 jit_solution(13561486433452275139)
XLA Ops:
  0.6 0.9 %pad_maximum_fusion.4 = f32[3,8,16,128]{3,2,1,0:T(8,128)S(1)} fusion(f32[1,8,16,128]{3,2,1,0:T(8,128)} %bitcast.128, f32[1,8,16,128]{3,2,1,0:T(8,128)} %bitcast.136, f32[1,8,16,128]{3,2,1,0:T(8,128)} %bitcast.144), kind=kLoop, calls=%fused_computation.35 | loop fusion | flops 98304 | bytes 393216 | tf_op jit(solution)/shard_map/stack | solution.py:124
  1.6 2.5 %collective-permute-start = (f32[3,4,16,128]{3,2,1,0:T(8,128)S(1)}, f32[3,4,16,128]{3,2,1,0:T(8,128)S(1)}, u32[]{:S(2)}, u32[]{:S(2)}) collective-permute-start(f32[3,4,16,128]{3,2,1,0:T(8,128)S(1)} %get-tuple-element.9), channel_id=1, source_target_pairs={{8,0},{16,8},{24,16},{0,24},{9,1},{17,9},{25,17},{1,25},{10,2},{18... | collective-permute-start | bytes 294920 | tf_op jit(solution)/shard_map/ppermute | solution.py:28
  4.2 3.7 %collective-permute-start.4 = (f32[2,8,16,4]{3,2,1,0:T(8,128)S(1)}, f32[2,8,16,4]{3,2,1,0:T(8,128)S(1)}, u32[]{:S(2)}, u32[]{:S(2)}) collective-permute-start(f32[2,8,16,4]{3,2,1,0:T(8,128)S(1)} %get-tuple-element.17), channel_id=1, source_target_pairs={{1,0},{2,1},{3,2},{0,3},{5,4},{6,5},{7,6},{4,7},{9,8},{10,9},{11,1... | collective-permute-start | bytes 12296 | tf_op jit(solution)/shard_map/ppermute | solution.py:28
  7.9 1.6 %collective-permute-start.2 = (f32[2,8,4,128]{3,2,1,0:T(4,128)S(1)}, f32[2,8,4,128]{3,2,1,0:T(4,128)S(1)}, u32[]{:S(2)}, u32[]{:S(2)}) collective-permute-start(f32[2,8,4,128]{3,2,1,0:T(4,128)S(1)} %get-tuple-element.13), channel_id=1, source_target_pairs={{4,0},{0,4},{5,1},{1,5},{6,2},{2,6},{7,3},{3,7},{12,8},{8,12},{13,... | collective-permute-start | bytes 98312 | tf_op jit(solution)/shard_map/ppermute | solution.py:28
  9.4 0.6 fusion.109
  10.1 0.7 fusion.102
  10.7 0.5 fusion.86
  11.3 0.5 fusion.84
  11.8 0.5 fusion.7
  12.3 0.6 fusion.97
  12.9 0.6 fusion.112
  13.5 0.6 fusion.6
  14.1 0.6 fusion.4
  15.0 0.6 copy-done.3
  15.5 0.6 fusion.5
  16.9 39.2 %all-reduce = (f32[96]{0:T(128)S(1)}, f32[96]{0:T(128)S(1)}) all-reduce(f32[96]{0:T(128)S(1)} %convolution_bitcast_fusion.1, f32[96]{0:T(128)S(1)} %convolution_bitcast_fusion), channel_id=1, replica_groups=mesh['gx'=4,'gy'=2,'gz'=4] {'gx','gy','gz'}, use_global_device_ids=true, to_apply=%region_0.1 | all-reduce | flops 192 | bytes 1536 | tf_op jit(solution)/shard_map/psum | solution.py:96
  56.4 0.3 fusion.80
  56.7 0.3 fusion.78
  57.3 0.3 convolution_subtract_fusion.2
  57.8 0.3 fusion.117
  58.1 0.3 fusion.104
  58.4 0.6 add_reduce_fusion
  59.4 0.3 fusion.3
  59.8 0.3 fusion.123
  60.1 0.3 fusion.2
  61.1 0.3 fusion.1
  61.5 2.3 %collective-permute-start.3 = (f32[2,8,4,128]{3,2,1,0:T(4,128)S(1)}, f32[2,8,4,128]{3,2,1,0:T(4,128)S(1)}, u32[]{:S(2)}, u32[]{:S(2)}) collective-permute-start(f32[2,8,4,128]{3,2,1,0:T(4,128)S(1)} %get-tuple-element.14), channel_id=1, source_target_pairs={{0,4},{4,0},{1,5},{5,1},{2,6},{6,2},{3,7},{7,3},{8,12},{12,8},{9,1... | collective-permute-start | bytes 98312 | tf_op jit(solution)/shard_map/ppermute | solution.py:27
  64.0 1.7 %collective-permute-done.3 = f32[2,8,4,128]{3,2,1,0:T(4,128)S(1)} collective-permute-done((f32[2,8,4,128]{3,2,1,0:T(4,128)S(1)}, f32[2,8,4,128]{3,2,1,0:T(4,128)S(1)}, u32[]{:S(2)}, u32[]{:S(2)}) %collective-permute-start.3) | collective-permute-done | bytes 32800 | tf_op jit(solution)/shard_map/ppermute | solution.py:27
  65.9 0.7 fusion.68
  66.6 0.3 fusion.14
  66.9 0.7 %fusion.45 = f32[8,16,128]{2,1,0:T(8,128)} fusion(f32[2,8,16,128]{3,2,1,0:T(8,128)S(1)} %fusion.14, f32[16,16,128]{2,1,0:T(8,128)S(1)} %get-tuple-element.5, f32[8,16,128]{2,1,0:T(8,128)S(1)} %copy-done, f32[8,16,128]{2,1,0:T(8,128)S(1)} %copy-done.2), kind=kLoop, calls=%fused_computation.94 | loop fusion | flops 294912 | bytes 786432 | tf_op jit(solution)/shard_map/sub | solution.py:143
  67.6 0.7 fusion.56
  (43 shorter events, 2.9 us)
Async XLA Ops:
  1.6 2.5 %copy-start = (f32[8,16,128]{2,1,0:T(8,128)S(1)}, f32[8,16,128]{2,1,0:T(8,128)}, u32[]{:S(2)}) copy-start(f32[8,16,128]{2,1,0:T(8,128)} %param.6) | copy-start | bytes 196612
  1.6 2.5 %copy-start.1 = (f32[8,16,128]{2,1,0:T(8,128)S(1)}, f32[8,16,128]{2,1,0:T(8,128)}, u32[]{:S(2)}) copy-start(f32[8,16,128]{2,1,0:T(8,128)} %param.5) | copy-start | bytes 196612
  1.6 64.2 %collective-permute-start = (f32[3,4,16,128]{3,2,1,0:T(8,128)S(1)}, f32[3,4,16,128]{3,2,1,0:T(8,128)S(1)}, u32[]{:S(2)}, u32[]{:S(2)}) collective-permute-start(f32[3,4,16,128]{3,2,1,0:T(8,128)S(1)} %get-tuple-element.9), channel_id=1, source_target_pairs={{8,0},{16,8},{24,16},{0,24},{9,1},{17,9},{25,17},{1,25},{10,2},{18... | collective-permute-start | bytes 294920 | tf_op jit(solution)/shard_map/ppermute | solution.py:28
  4.1 61.7 %collective-permute-start.1 = (f32[3,4,16,128]{3,2,1,0:T(8,128)S(1)}, f32[3,4,16,128]{3,2,1,0:T(8,128)S(1)}, u32[]{:S(2)}, u32[]{:S(2)}) collective-permute-start(f32[3,4,16,128]{3,2,1,0:T(8,128)S(1)} %get-tuple-element.10), channel_id=1, source_target_pairs={{0,8},{8,16},{16,24},{24,0},{1,9},{9,17},{17,25},{25,1},{2,10},{10... | collective-permute-start | bytes 294920 | tf_op jit(solution)/shard_map/ppermute | solution.py:27
  4.2 57.3 %collective-permute-start.4 = (f32[2,8,16,4]{3,2,1,0:T(8,128)S(1)}, f32[2,8,16,4]{3,2,1,0:T(8,128)S(1)}, u32[]{:S(2)}, u32[]{:S(2)}) collective-permute-start(f32[2,8,16,4]{3,2,1,0:T(8,128)S(1)} %get-tuple-element.17), channel_id=1, source_target_pairs={{1,0},{2,1},{3,2},{0,3},{5,4},{6,5},{7,6},{4,7},{9,8},{10,9},{11,1... | collective-permute-start | bytes 12296 | tf_op jit(solution)/shard_map/ppermute | solution.py:28
  7.9 1.6 %copy-start.2 = (f32[8,16,128]{2,1,0:T(8,128)S(1)}, f32[8,16,128]{2,1,0:T(8,128)}, u32[]{:S(2)}) copy-start(f32[8,16,128]{2,1,0:T(8,128)} %param.4) | copy-start | bytes 196612
  7.9 56.0 %collective-permute-start.5 = (f32[2,8,16,4]{3,2,1,0:T(8,128)S(1)}, f32[2,8,16,4]{3,2,1,0:T(8,128)S(1)}, u32[]{:S(2)}, u32[]{:S(2)}) collective-permute-start(f32[2,8,16,4]{3,2,1,0:T(8,128)S(1)} %get-tuple-element.18), channel_id=1, source_target_pairs={{0,1},{1,2},{2,3},{3,0},{4,5},{5,6},{6,7},{7,4},{8,9},{9,10},{10,1... | collective-permute-start | bytes 12296 | tf_op jit(solution)/shard_map/ppermute | solution.py:27
  7.9 56.1 %collective-permute-start.2 = (f32[2,8,4,128]{3,2,1,0:T(4,128)S(1)}, f32[2,8,4,128]{3,2,1,0:T(4,128)S(1)}, u32[]{:S(2)}, u32[]{:S(2)}) collective-permute-start(f32[2,8,4,128]{3,2,1,0:T(4,128)S(1)} %get-tuple-element.13), channel_id=1, source_target_pairs={{4,0},{0,4},{5,1},{1,5},{6,2},{2,6},{7,3},{3,7},{12,8},{8,12},{13,... | collective-permute-start | bytes 98312 | tf_op jit(solution)/shard_map/ppermute | solution.py:28
  14.8 0.7 %copy-start.3 = (s32[96,3]{0,1:T(4,128)S(1)}, s32[96,3]{0,1:T(4,128)}, u32[]{:S(2)}) copy-start(s32[96,3]{0,1:T(4,128)} %param.7) | copy-start | bytes 3460
  61.5 4.2 %collective-permute-start.3 = (f32[2,8,4,128]{3,2,1,0:T(4,128)S(1)}, f32[2,8,4,128]{3,2,1,0:T(4,128)S(1)}, u32[]{:S(2)}, u32[]{:S(2)}) collective-permute-start(f32[2,8,4,128]{3,2,1,0:T(4,128)S(1)} %get-tuple-element.14), channel_id=1, source_target_pairs={{0,4},{4,0},{1,5},{5,1},{2,6},{6,2},{3,7},{7,3},{8,12},{12,8},{9,1... | collective-permute-start | bytes 98312 | tf_op jit(solution)/shard_map/ppermute | solution.py:27
where the time goes:
time: 68.6 us; the launch traced here: 68.3 us
  blocking collectives  39.2 us (57%)
  starting transfers between devices  10.1 us (15%)
  matrix products  9.66 us (14%)
  other arithmetic  4.3 us (6%)
  local copies, waits for them, and re-layouts  1.83 us (3%)
  waiting for transfers between devices  1.76 us (3%)
  between operations  1.52 us (2%)
    psum x1, blocking collectives, modal_force(): summed = lax.psum((local_cos, local_sin), ('gx', 'gy', 'gz'))  39.2 us
    ppermute x3, starting transfers between devices, padded_2(): after = lax.ppermute(first, axis, down)  7.7 us
    ppermute x3, starting transfers between devices, padded_2(): before = lax.ppermute(last, axis, up)  2.35 us
    ppermute x3, waiting for transfers between devices, padded_2(): before = lax.ppermute(last, axis, up)  1.75 us
  transfers between devices with their start and end apart: 6, of which 1 were waited for; matrix products, arithmetic and copies ran while one was open for 17% of the time, Pallas kernels for 0%

commit v1 on v0

v1 whole, which is shorter than its diff:
```python
import functools
import math

import jax
import jax.numpy as jnp
import numpy as np
from jax import lax
from jax.experimental import pallas as pl
from jax.experimental.pallas import tpu as pltpu
from jax.sharding import PartitionSpec as P

KMAX = 3
WIDTH = 2 * KMAX + 1
HALF = 64
REACH = 4

FIRST_COEFFS = (0.8, -0.2, 4.0 / 105.0, -1.0 / 280.0)
SECOND_COEFFS = (1.6, -0.2, 8.0 / 315.0, -1.0 / 560.0)
CENTRE_COEFF = -205.0 / 72.0
VISCOSITY = 0.3
DIFFUSIVITY = 1.5
FORCE_POWER = 0.3
ENERGY_EPS = 1e-06
ACTIVATION = 2.0
HIGHEST = lax.Precision.HIGHEST
MESH = pl.DeviceIdType.MESH


def tables(local, full):
    size_x, size_y, size_z = local
    full_x, full_y, full_z = full
    k = np.arange(-KMAX, KMAX + 1)
    ang_z = 2.0 * np.pi * (k[:, None] * np.arange(size_z)[None, :]) / full_z
    trig_z = np.zeros((16, size_z))
    trig_z[:WIDTH] = np.cos(ang_z)
    trig_z[8 : 8 + WIDTH] = np.sin(ang_z)
    ax = k[:, None] * np.arange(size_x)[None, :] / full_x
    ay = k[:, None] * np.arange(size_y)[None, :] / full_y
    ang = 2.0 * np.pi * (ax[:, None, :, None] + ay[None, :, None, :])
    ang = ang.reshape(WIDTH * WIDTH, size_x * size_y)
    trig_xy = np.zeros((2 * HALF, size_x * size_y))
    trig_xy[: WIDTH * WIDTH] = np.cos(ang)
    trig_xy[HALF : HALF + WIDTH * WIDTH] = np.sin(ang)
    edge = np.zeros((8, size_z))
    for j in range(REACH):
        edge[j, j] = 1.0
        edge[REACH + j, size_z - REACH + j] = 1.0
    band = np.zeros((size_z, size_z))
    halo = np.zeros((16, size_z))
    for z in range(size_z):
        band[z, z] = 3.0 * CENTRE_COEFF
        for offset, weight in enumerate(SECOND_COEFFS, 1):
            for q in (z - offset, z + offset):
                if 0 <= q < size_z:
                    band[q, z] = weight
                elif q < 0:
                    halo[8 + q, z] = weight
                else:
                    halo[8 + q - size_z, z] = weight
    early = np.concatenate([trig_z, edge, trig_xy], 0).astype(np.float32)
    late = np.concatenate([halo, band], 0).astype(np.float32)
    return early, late


def dot_nt(a, b):
    return lax.dot_general(a, b, (((1,), (1,)), ((), ())), precision=HIGHEST, preferred_element_type=jnp.float32)


def dot_nn(a, b):
    return lax.dot_general(a, b, (((1,), (0,)), ((), ())), precision=HIGHEST, preferred_element_type=jnp.float32)


def dot_tn(a, b):
    return lax.dot_general(a, b, (((0,), (0,)), ((), ())), precision=HIGHEST, preferred_element_type=jnp.float32)


def group_offsets(sizes, axes):
    offsets = [{}]
    for axis in axes:
        offsets = [{**o, axis: s} for o in offsets for s in range(sizes[axis])]
    return [o for o in offsets if any(o.values())]


def tree_sum(parts):
    parts = list(parts)
    while len(parts) > 1:
        parts = [sum(parts[i : i + 2][1:], parts[i]) for i in range(0, len(parts), 2)]
    return parts[0]


def plan(sizes):
    if sizes["gx"] * sizes["gy"] <= 16:
        stages = [("gz",), ("gx", "gy")]
    else:
        stages = [("gz",), ("gx",), ("gy",)]
    return [group_offsets(sizes, s) for s in stages]


def kernel(sizes, local, dens_hbm, mom_hbm, fuel_hbm, modes_hbm, early_hbm, late_hbm,
           drate_hbm, mrate_hbm, hrate_hbm,
           f, modes, early, late, edges, sides, ypack, zpack, ztile, stage_own, stage_got, outs,
           load_sem, store_sem, halo_send, halo_recv, stage_send, stage_recv):
    size_x, size_y, size_z = local
    rows = size_x * size_y
    me = {a: lax.axis_index(a) for a in sizes}
    stages = plan(sizes)

    def at(offset):
        return {a: lax.rem(me[a] + o, sizes[a]) for a, o in offset.items()}

    own = pl.ds(REACH, size_x)
    loads = [
        pltpu.make_async_copy(src, dst, load_sem.at[i])
        for i, (src, dst) in enumerate([
            (dens_hbm, f.at[0, own]), (mom_hbm, f.at[1, own]), (early_hbm, early),
            (fuel_hbm, f.at[2, own]), (modes_hbm, modes), (late_hbm, late),
        ])
    ]
    for copy in loads:
        copy.start()
    barrier = pltpu.get_barrier_semaphore()
    partners = [o for group in stages for o in group]
    for offset in partners:
        pl.semaphore_signal(barrier, inc=1, device_id=at(offset), device_id_type=MESH)

    row = lax.broadcasted_iota(jnp.int32, (8, 2 * HALF), 0)
    lane = lax.broadcasted_iota(jnp.int32, (8, 2 * HALF), 1)
    pair = lax.rem(lane, HALF)
    kx = lax.div(pair, WIDTH)
    ky = pair - kx * WIDTH
    turn = jnp.zeros((8, 2 * HALF), jnp.float32)
    for k, axis, size in ((kx, "gx", size_x), (ky, "gy", size_y), (row, "gz", size_z)):
        count = (k - KMAX).astype(jnp.float32) * me[axis].astype(jnp.float32)
        part = count / sizes[axis]
        turn = turn + (part - jnp.floor(part))
    turn = turn - jnp.floor(turn + 0.5)
    cos_p = jnp.cos(2.0 * math.pi * turn)
    sin_p = jnp.sin(2.0 * math.pi * turn)
    sign = jnp.where(lane < HALF, -1.0, 1.0)
    sin_p = sign * sin_p

    loads[0].wait()
    loads[1].wait()
    loads[2].wait()
    flat = lambda i: f[i, own].reshape(rows, size_z)
    vel = flat(1) / flat(0)
    trig_z = early[0:16]
    trig_xy = early[24 : 24 + 2 * HALF]
    grid = dot_nt(dot_nt(trig_z, vel), trig_xy)
    cube = grid[0:8] + sign * pltpu.roll(grid[8:16], HALF, 1)
    cube = cos_p * cube + sin_p * pltpu.roll(cube, HALF, 1)
    stage_own[0] = cube

    def send_stage(s):
        base = sum(len(g) for g in stages[:s])
        copies = []
        for i, offset in enumerate(stages[s]):
            copy = pltpu.make_async_remote_copy(
                src_ref=stage_own.at[s], dst_ref=stage_got.at[base + i],
                send_sem=stage_send.at[base + i], recv_sem=stage_recv.at[base + i],
                device_id=at(offset), device_id_type=MESH)
            copy.start()
            copies.append(copy)
        return copies

    def sum_stage(s, copies):
        base = sum(len(g) for g in stages[:s])
        for copy in copies:
            copy.wait_recv()
        return tree_sum([stage_own[s]] + [stage_got[base + i] for i in range(len(copies))])

    pl.semaphore_wait(barrier, len(partners))
    pending = send_stage(0)
    started = list(pending)
    loads[3].wait()

    def send(src, dst, slot, axis, step):
        copy = pltpu.make_async_remote_copy(
            src_ref=src, dst_ref=dst, send_sem=halo_send.at[slot], recv_sem=halo_recv.at[slot],
            device_id=at({axis: step % sizes[axis]}), device_id_type=MESH)
        copy.start()
        return copy

    halos_x = [
        send(f.at[:, pl.ds(size_x, REACH)], f.at[:, pl.ds(0, REACH)], 0, "gx", 1),
        send(f.at[:, pl.ds(REACH, REACH)], f.at[:, pl.ds(size_x + REACH, REACH)], 1, "gx", -1),
    ]
    for i in range(2):
        ypack[i, :, 0:REACH] = f[1 + i, own, 0:REACH]
        ypack[i, :, REACH : 2 * REACH] = f[1 + i, own, size_y - REACH : size_y]
        zpack[i] = dot_nt(early[16:24], flat(1 + i))
    halos_y = [send(ypack, sides.at[0], 2, "gy", 1)]
    if sizes["gy"] > 2:
        halos_y.append(send(ypack, sides.at[1], 3, "gy", -1))
    halos_z = [send(zpack, ztile.at[0], 4, "gz", 1), send(zpack, ztile.at[1], 5, "gz", -1)]

    loads[4].wait()
    hit_z = lax.broadcasted_iota(jnp.int32, (8, modes.shape[1]), 0) == modes[2:3] + KMAX
    code = (modes[0:1] + KMAX) * WIDTH + modes[1:2] + KMAX
    hit_xy = lax.rem(lax.broadcasted_iota(jnp.int32, (2 * HALF, modes.shape[1]), 0), HALF) == code
    chosen = dot_nt(hit_z.astype(jnp.float32), hit_xy.astype(jnp.float32))

    loads[5].wait()
    lap = [dot_nn(flat(1 + i), late[16 : 16 + size_z]).reshape(size_x, size_y, size_z) for i in range(2)]
    outs[1] = lap[0]
    outs[2] = lap[1]

    for s in range(1, len(stages)):
        stage_own[s] = sum_stage(s - 1, pending)
        pending = send_stage(s)
        started += pending

    for copy in halos_z:
        copy.wait_recv()
    for copy in halos_y:
        copy.wait_recv()
    for i in range(2):
        tile = jnp.concatenate([ztile[0, i], ztile[1, i]], 0)
        edges[i, :, 0:8] = sides[0, i]
        edges[i, :, 8 : 8 + size_y] = f[1 + i, own]
        edges[i, :, 8 + size_y : 16 + size_y] = sides[1 if sizes["gy"] > 2 else 0, i]
        total = outs[1 + i] + dot_tn(tile, late[0:16]).reshape(size_x, size_y, size_z)
        for offset, weight in enumerate(SECOND_COEFFS, 1):
            total = total + weight * (
                edges[i, :, 8 + offset : 8 + offset + size_y] + edges[i, :, 8 - offset : 8 - offset + size_y])
        outs[1 + i] = total

    for copy in halos_x:
        copy.wait_recv()
    def planes(x, offset):
        return x[REACH + offset : REACH + offset + size_x]

    def first_diff(x):
        total = None
        for offset, weight in enumerate(FIRST_COEFFS, 1):
            term = weight * (planes(x, offset) - planes(x, -offset))
            total = term if total is None else total + term
        return total

    def second_diff(x):
        return tree_sum([w * (planes(x, o) + planes(x, -o)) for o, w in enumerate(SECOND_COEFFS, 1)])

    mom = f[1]
    dens = f[0]
    fuel = f[2]
    vel_pad = mom / dens
    outs[0] = -first_diff(mom)
    stores = [pltpu.make_async_copy(outs.at[0], drate_hbm, store_sem.at[0])]
    stores[0].start()
    mid_fuel = planes(fuel, 0)
    outs[2] = (DIFFUSIVITY * (outs[2] + second_diff(fuel)) - first_diff(fuel * vel_pad)
               - mid_fuel * jnp.exp(-ACTIVATION * mid_fuel / planes(dens, 0)))
    stores.append(pltpu.make_async_copy(outs.at[2], hrate_hbm, store_sem.at[1]))
    stores[1].start()
    outs[1] = VISCOSITY * (outs[1] + second_diff(mom)) - first_diff(mom * vel_pad + dens)

    ncell = float(rows * size_z * math.prod(sizes.values()))
    cube = sum_stage(len(stages) - 1, pending)
    coef = chosen * cube / ncell
    energy = jnp.sum(jnp.sum(coef * coef, axis=1, keepdims=True), axis=0, keepdims=True)
    scale = 2.0 * FORCE_POWER / (energy + ENERGY_EPS)
    local_coef = cos_p * coef - sin_p * pltpu.roll(coef, HALF, 1)
    both = jnp.concatenate([local_coef, -sign * pltpu.roll(local_coef, HALF, 1)], 0)
    low = dot_tn(dot_nn(both, trig_xy), trig_z).reshape(size_x, size_y, size_z)
    outs[1] = outs[1] + f[0, own] * (low * scale.reshape(1, 1, 1))
    stores.append(pltpu.make_async_copy(outs.at[1], mrate_hbm, store_sem.at[2]))
    stores[2].start()
    for copy in started + halos_x + halos_y + halos_z:
        copy.wait_send()
    for copy in stores:
        copy.wait()


def solution(mesh):
    sizes = {a: mesh.shape[a] for a in ("gx", "gy", "gz")}

    def per_device(density, momentum, hydrogen, forced_modes):
        local = density.shape
        size_x, size_y, size_z = local
        rows = size_x * size_y
        full = (size_x * sizes["gx"], size_y * sizes["gy"], size_z * sizes["gz"])
        early, late = tables(local, full)
        modes = forced_modes.T
        stages = plan(sizes)
        messages = sum(len(g) for g in stages)
        any_spec = pl.BlockSpec(memory_space=pl.ANY)
        f32 = jnp.float32
        return tuple(pl.pallas_call(
            functools.partial(kernel, sizes, local),
            out_shape=[jax.ShapeDtypeStruct(local, f32)] * 3,
            in_specs=[any_spec] * 6,
            out_specs=[any_spec] * 3,
            scratch_shapes=[
                pltpu.VMEM((3, size_x + 2 * REACH, size_y, size_z), f32),
                pltpu.VMEM(modes.shape, jnp.int32),
                pltpu.VMEM(early.shape, f32),
                pltpu.VMEM(late.shape, f32),
                pltpu.VMEM((2, size_x, size_y + 16, size_z), f32),
                pltpu.VMEM((2, 2, size_x, 8, size_z), f32),
                pltpu.VMEM((2, size_x, 8, size_z), f32),
                pltpu.VMEM((2, 8, rows), f32),
                pltpu.VMEM((2, 2, 8, rows), f32),
                pltpu.VMEM((len(stages), 8, 2 * HALF), f32),
                pltpu.VMEM((messages, 8, 2 * HALF), f32),
                pltpu.VMEM((3,) + tuple(local), f32),
                pltpu.SemaphoreType.DMA((6,)),
                pltpu.SemaphoreType.DMA((3,)),
                pltpu.SemaphoreType.DMA((6,)),
                pltpu.SemaphoreType.DMA((6,)),
                pltpu.SemaphoreType.DMA((messages,)),
                pltpu.SemaphoreType.DMA((messages,)),
            ],
            compiler_params=pltpu.CompilerParams(collective_id=0, has_side_effects=True),
            name="flame",
        )(density, momentum, hydrogen, modes, jnp.asarray(early), jnp.asarray(late)))

    in_specs = (P("gx", "gy", "gz"), P("gx", "gy", "gz"), P("gx", "gy", "gz"), P())
    out_specs = (P("gx", "gy", "gz"), P("gx", "gy", "gz"), P("gx", "gy", "gz"))
    return jax.shard_map(
        per_device, mesh=mesh, in_specs=in_specs, out_specs=out_specs, check_vma=False
    )
```

time: 68.6 us -> 18.1 us (0.26)
  blocking collectives: 39.2 us -> 0 us
  Pallas kernels: 0 us -> 14.1 us
  starting transfers between devices: 10.1 us -> 0 us
  matrix products: 9.66 us -> 0 us
  other arithmetic: 4.3 us -> 0 us
  waiting for transfers between devices: 1.76 us -> 0 us
  local copies, waits for them, and re-layouts: 1.83 us -> 3 us
  between operations: 1.52 us -> 0.65 us
    psum x1 -> x0, blocking collectives: 39.2 us -> none  [modal_force(): summed = lax.psum((local_cos, local_sin), ('gx', 'gy', 'gz'))]
    pallas_call x0 -> x1, Pallas kernels: none -> 14.1 us  [per_device(): pl.pallas_call(functools.partial(kernel, sizes, local), out_shape=[jax.Sh...]
    ppermute x6 -> x0, starting transfers between devices: 10.1 us -> none  [the longest x3 7.7 us: padded_2(): after = lax.ppermute(first, axis, down)]
    dot_general x24 -> x0, matrix products: 9.66 us -> none  [the longest x1 0.66 us: modal_force(): lax.dot_general(sin_z, flat, contract, precision=HIGHEST)]
    unnamed x8 -> x7, local copies, waits for them, and re-layouts: 0.58 us -> 3 us
    ppermute x6 -> x0, waiting for transfers between devices: 1.76 us -> none  [the longest x3 1.75 us: padded_2(): before = lax.ppermute(last, axis, up)]
    another operation x3 -> x0, other arithmetic: 1.02 us -> none  [stencil_terms(): fields = jnp.stack([density, momentum, hydrogen])]
    add x6 -> x0, other arithmetic: 1.02 us -> none  [the longest x1 0.67 us: per_device(): momentum_rate = momentum_part + density * force]
  transfers between devices with their start and end apart: 6 -> 0, of which waited for: 1 -> 0; matrix products, arithmetic and copies ran while one was open for 17% -> 0% of each run, Pallas kernels for 0% -> 0%
where the time goes in v1:
time: 18.1 us; the launch traced here: 17.8 us
  Pallas kernels  14.1 us (78%)
  local copies, waits for them, and re-layouts  3 us (17%)
  between operations  0.65 us (4%)
    pallas_call x1, Pallas kernels, per_device(): pl.pallas_call(functools.partial(kernel, sizes, local), out_shape=[jax.Sh...  14.1 us
    unnamed x7, local copies, waits for them, and re-layouts  3 us

profile of v1, /device:TPU:0, one launch (start us, length us, event | category | flops | bytes accessed | tf_op | source)
XLA Modules:
  0.0 17.8 jit_solution(5068638298426453174)
XLA Ops:
  0.6 14.1 %flame.1 = (f32[8,16,128]{2,1,0:T(8,128)}, f32[8,16,128]{2,1,0:T(8,128)}, f32[8,16,128]{2,1,0:T(8,128)}) custom-call(f32[8,16,128]{2,1,0:T(8,128)} %dens_hbm.1, f32[8,16,128]{2,1,0:T(8,128)} %mom_hbm.1, f32[8,16,128]{2,1,0:T(8,128)} %fuel_hbm.1, s32[3,96]{1,0:T(4,128)} %bitcast.1, f32[152,128]{1,0:T(8,128)} %constant.4.clone.early_hbm, ...), custom_call_target="tpu_custom_call" | custom-call | tf_op jit(solution)/shard_map/flame/pallas_call | solution.py:288
  14.8 0.0 copy-start.1
  14.8 1.5 %copy.12 = f32[8,16,128]{2,1,0:T(8,128)} copy(f32[8,16,128]{2,1,0:T(8,128)} %get-tuple-element.6) | data formatting | bytes 131072
  16.3 0.0 copy-done.1
  16.3 0.0 copy-start
  16.3 0.6 %copy.13 = f32[8,16,128]{2,1,0:T(8,128)} copy(f32[8,16,128]{2,1,0:T(8,128)S(1)} %copy-done.1) | data formatting | bytes 131072
  16.9 0.2 %copy-done = f32[8,16,128]{2,1,0:T(8,128)S(1)} copy-done((f32[8,16,128]{2,1,0:T(8,128)S(1)}, f32[8,16,128]{2,1,0:T(8,128)}, u32[]{:S(2)}) %copy-start) | copy-done | bytes 65560
  17.2 0.6 %copy.14 = f32[8,16,128]{2,1,0:T(8,128)} copy(f32[8,16,128]{2,1,0:T(8,128)S(1)} %copy-done) | data formatting | bytes 131072
Async XLA Ops:
  14.8 1.5 %copy-start.1 = (f32[8,16,128]{2,1,0:T(8,128)S(1)}, f32[8,16,128]{2,1,0:T(8,128)}, u32[]{:S(2)}) copy-start(f32[8,16,128]{2,1,0:T(8,128)} %get-tuple-element.7) | copy-start | bytes 196612
  16.3 0.9 %copy-start = (f32[8,16,128]{2,1,0:T(8,128)S(1)}, f32[8,16,128]{2,1,0:T(8,128)}, u32[]{:S(2)}) copy-start(f32[8,16,128]{2,1,0:T(8,128)} %get-tuple-element.8) | copy-start | bytes 196612

commit v2 on v1

--- a/solution.py
+++ b/solution.py
@@ -97,9 +97,9 @@
 
 
 def kernel(sizes, local, dens_hbm, mom_hbm, fuel_hbm, modes_hbm, early_hbm, late_hbm,
-           drate_hbm, mrate_hbm, hrate_hbm,
-           f, modes, early, late, edges, sides, ypack, zpack, ztile, stage_own, stage_got, outs,
-           load_sem, store_sem, halo_send, halo_recv, stage_send, stage_recv):
+           drate, mrate, hrate,
+           f, modes, early, late, edges, sides, ypack, zpack, ztile, stage_own, stage_got,
+           load_sem, halo_send, halo_recv, stage_send, stage_recv):
     size_x, size_y, size_z = local
     rows = size_x * size_y
     me = {a: lax.axis_index(a) for a in sizes}
@@ -202,8 +202,9 @@
 
     loads[5].wait()
     lap = [dot_nn(flat(1 + i), late[16 : 16 + size_z]).reshape(size_x, size_y, size_z) for i in range(2)]
-    outs[1] = lap[0]
-    outs[2] = lap[1]
+    outs = (drate, mrate, hrate)
+    mrate[...] = lap[0]
+    hrate[...] = lap[1]
 
     for s in range(1, len(stages)):
         stage_own[s] = sum_stage(s - 1, pending)
@@ -219,11 +220,11 @@
         edges[i, :, 0:8] = sides[0, i]
         edges[i, :, 8 : 8 + size_y] = f[1 + i, own]
         edges[i, :, 8 + size_y : 16 + size_y] = sides[1 if sizes["gy"] > 2 else 0, i]
-        total = outs[1 + i] + dot_tn(tile, late[0:16]).reshape(size_x, size_y, size_z)
+        total = outs[1 + i][...] + dot_tn(tile, late[0:16]).reshape(size_x, size_y, size_z)
         for offset, weight in enumerate(SECOND_COEFFS, 1):
             total = total + weight * (
                 edges[i, :, 8 + offset : 8 + offset + size_y] + edges[i, :, 8 - offset : 8 - offset + size_y])
-        outs[1 + i] = total
+        outs[1 + i][...] = total
 
     for copy in halos_x:
         copy.wait_recv()
@@ -244,15 +245,11 @@
     dens = f[0]
     fuel = f[2]
     vel_pad = mom / dens
-    outs[0] = -first_diff(mom)
-    stores = [pltpu.make_async_copy(outs.at[0], drate_hbm, store_sem.at[0])]
-    stores[0].start()
+    drate[...] = -first_diff(mom)
     mid_fuel = planes(fuel, 0)
-    outs[2] = (DIFFUSIVITY * (outs[2] + second_diff(fuel)) - first_diff(fuel * vel_pad)
-               - mid_fuel * jnp.exp(-ACTIVATION * mid_fuel / planes(dens, 0)))
-    stores.append(pltpu.make_async_copy(outs.at[2], hrate_hbm, store_sem.at[1]))
-    stores[1].start()
-    outs[1] = VISCOSITY * (outs[1] + second_diff(mom)) - first_diff(mom * vel_pad + dens)
+    hrate[...] = (DIFFUSIVITY * (hrate[...] + second_diff(fuel)) - first_diff(fuel * vel_pad)
+                  - mid_fuel * jnp.exp(-ACTIVATION * mid_fuel / planes(dens, 0)))
+    mrate[...] = VISCOSITY * (mrate[...] + second_diff(mom)) - first_diff(mom * vel_pad + dens)
 
     ncell = float(rows * size_z * math.prod(sizes.values()))
     cube = sum_stage(len(stages) - 1, pending)
@@ -262,12 +259,17 @@
     local_coef = cos_p * coef - sin_p * pltpu.roll(coef, HALF, 1)
     both = jnp.concatenate([local_coef, -sign * pltpu.roll(local_coef, HALF, 1)], 0)
     low = dot_tn(dot_nn(both, trig_xy), trig_z).reshape(size_x, size_y, size_z)
-    outs[1] = outs[1] + f[0, own] * (low * scale.reshape(1, 1, 1))
-    stores.append(pltpu.make_async_copy(outs.at[1], mrate_hbm, store_sem.at[2]))
-    stores[2].start()
+    mrate[...] = mrate[...] + f[0, own] * (low * scale.reshape(1, 1, 1))
     for copy in started + halos_x + halos_y + halos_z:
         copy.wait_send()
-    for copy in stores:
+
+
+def write_out(*refs):
+    count = len(refs) // 2
+    copies = [pltpu.make_async_copy(refs[i], refs[count + i], refs[-1].at[i]) for i in range(count)]
+    for copy in copies:
+        copy.start()
+    for copy in copies:
         copy.wait()
 
 
@@ -285,11 +287,11 @@
         messages = sum(len(g) for g in stages)
         any_spec = pl.BlockSpec(memory_space=pl.ANY)
         f32 = jnp.float32
-        return tuple(pl.pallas_call(
+        rates = pl.pallas_call(
             functools.partial(kernel, sizes, local),
-            out_shape=[jax.ShapeDtypeStruct(local, f32)] * 3,
+            out_shape=[pltpu.VMEM(local, f32)] * 3,
             in_specs=[any_spec] * 6,
-            out_specs=[any_spec] * 3,
+            out_specs=[pl.BlockSpec(memory_space=pltpu.VMEM)] * 3,
             scratch_shapes=[
                 pltpu.VMEM((3, size_x + 2 * REACH, size_y, size_z), f32),
                 pltpu.VMEM(modes.shape, jnp.int32),
@@ -302,9 +304,7 @@
                 pltpu.VMEM((2, 2, 8, rows), f32),
                 pltpu.VMEM((len(stages), 8, 2 * HALF), f32),
                 pltpu.VMEM((messages, 8, 2 * HALF), f32),
-                pltpu.VMEM((3,) + tuple(local), f32),
                 pltpu.SemaphoreType.DMA((6,)),
-                pltpu.SemaphoreType.DMA((3,)),
                 pltpu.SemaphoreType.DMA((6,)),
                 pltpu.SemaphoreType.DMA((6,)),
                 pltpu.SemaphoreType.DMA((messages,)),
@@ -312,7 +312,15 @@
             ],
             compiler_params=pltpu.CompilerParams(collective_id=0, has_side_effects=True),
             name="flame",
-        )(density, momentum, hydrogen, modes, jnp.asarray(early), jnp.asarray(late)))
+        )(density, momentum, hydrogen, modes, jnp.asarray(early), jnp.asarray(late))
+        return tuple(pl.pallas_call(
+            write_out,
+            out_shape=[jax.ShapeDtypeStruct(local, f32)] * 3,
+            in_specs=[pl.BlockSpec(memory_space=pltpu.VMEM)] * 3,
+            out_specs=[any_spec] * 3,
+            scratch_shapes=[pltpu.SemaphoreType.DMA((3,))],
+            name="write",
+        )(*[pltpu.with_memory_space_constraint(r, pltpu.VMEM) for r in rates]))
 
     in_specs = (P("gx", "gy", "gz"), P("gx", "gy", "gz"), P("gx", "gy", "gz"), P())
     out_specs = (P("gx", "gy", "gz"), P("gx", "gy", "gz"), P("gx", "gy", "gz"))

time: 18.1 us -> 15 us (0.83)
  local copies, waits for them, and re-layouts: 3 us -> 0 us
    unnamed x7 -> x0, local copies, waits for them, and re-layouts: 3 us -> none
    pallas_call x1 -> x2, Pallas kernels: 14.1 us -> 14.2 us  [the longest x1 13.5 us: per_device(): pl.pallas_call(functools.partial(kernel, sizes, local), out_shape=[pltpu....]
where the time goes in v2:
time: 15 us; the launch traced here: 14.9 us
  Pallas kernels  14.2 us (95%)
  between operations  0.64 us (4%)
    pallas_call x1, Pallas kernels, per_device(): pl.pallas_call(functools.partial(kernel, sizes, local), out_shape=[pltpu....  13.5 us
    pallas_call x1, Pallas kernels, per_device(): pl.pallas_call(write_out, out_shape=[jax.ShapeDtypeStruct(local, f32)] *...  0.7 us

profile of v2, /device:TPU:0, one launch (start us, length us, event | category | flops | bytes accessed | tf_op | source)
XLA Modules:
  0.0 14.9 jit_solution(6866149200013992463)
XLA Ops:
  0.6 13.5 %flame.1 = (f32[8,16,128]{2,1,0:T(8,128)S(1)}, f32[8,16,128]{2,1,0:T(8,128)S(1)}, f32[8,16,128]{2,1,0:T(8,128)S(1)}) custom-call(f32[8,16,128]{2,1,0:T(8,128)} %dens_hbm.1, f32[8,16,128]{2,1,0:T(8,128)} %mom_hbm.1, f32[8,16,128]{2,1,0:T(8,128)} %fuel_hbm.1, s32[3,96]{1,0:T(4,128)} %bitcast.1, f32[152,128]{1,0:T(8,128)} %constant.4.clone.early_hbm, ...), custom_call_target="tpu_custom_call" | custom-call | tf_op jit(solution)/shard_map/flame/pallas_call | solution.py:290
  14.2 0.7 %write.1 = (f32[8,16,128]{2,1,0:T(8,128)}, f32[8,16,128]{2,1,0:T(8,128)}, f32[8,16,128]{2,1,0:T(8,128)}) custom-call(f32[8,16,128]{2,1,0:T(8,128)S(1)} %get-tuple-element.6.refs_0_, f32[8,16,128]{2,1,0:T(8,128)S(1)} %get-tuple-element.7.refs_1_, f32[8,16,128]{2,1,0:T(8,128)S(1)} %get-tuple-element.8.refs_2_), custom_call_target="tpu_custom_call" | custom-call | tf_op jit(solution)/shard_map/write/pallas_call | solution.py:316

commit v3 on v2

--- a/solution.py
+++ b/solution.py
@@ -12,6 +12,7 @@
 KMAX = 3
 WIDTH = 2 * KMAX + 1
 HALF = 64
+ROWS = KMAX + 1
 REACH = 4
 
 FIRST_COEFFS = (0.8, -0.2, 4.0 / 105.0, -1.0 / 280.0)
@@ -31,9 +32,9 @@
     full_x, full_y, full_z = full
     k = np.arange(-KMAX, KMAX + 1)
     ang_z = 2.0 * np.pi * (k[:, None] * np.arange(size_z)[None, :]) / full_z
-    trig_z = np.zeros((16, size_z))
-    trig_z[:WIDTH] = np.cos(ang_z)
-    trig_z[8 : 8 + WIDTH] = np.sin(ang_z)
+    trig_z = np.zeros((2 * ROWS, size_z))
+    trig_z[:ROWS] = np.cos(ang_z[KMAX:])
+    trig_z[ROWS:] = np.sin(ang_z[KMAX:])
     ax = k[:, None] * np.arange(size_x)[None, :] / full_x
     ay = k[:, None] * np.arange(size_y)[None, :] / full_y
     ang = 2.0 * np.pi * (ax[:, None, :, None] + ay[None, :, None, :])
@@ -57,9 +58,34 @@
                     halo[8 + q, z] = weight
                 else:
                     halo[8 + q - size_z, z] = weight
-    early = np.concatenate([trig_z, edge, trig_xy], 0).astype(np.float32)
-    late = np.concatenate([halo, band], 0).astype(np.float32)
-    return early, late
+    z_high, z_low = split_host(trig_z)
+    xy_high, xy_low = split_host(trig_xy)
+    early = np.concatenate([z_high, z_low, xy_high, xy_low, z_high, z_high, z_low, z_low], 0)
+    back = np.concatenate([xy_high, xy_low], 1)
+    late = np.concatenate([edge, halo, band], 0).astype(np.float32)
+    return early, back, late
+
+
+def split_host(table):
+    high = table.astype(np.float32).astype(jnp.bfloat16)
+    low = (table - high.astype(np.float64)).astype(np.float32).astype(jnp.bfloat16)
+    return high, low
+
+
+def split(x):
+    high = x.astype(jnp.bfloat16).astype(jnp.float32)
+    return high, x - high
+
+
+def dot_split(a, b, contract):
+    return lax.dot_general(a.astype(jnp.bfloat16), b.astype(jnp.bfloat16), (contract, ((), ())),
+                           preferred_element_type=jnp.float32)
+
+
+def fold(x):
+    rows, lanes = x.shape
+    x = x[: rows // 2] + x[rows // 2 :]
+    return x[:, : lanes // 2] + x[:, lanes // 2 :]
 
 
 def dot_nt(a, b):
@@ -96,12 +122,13 @@
     return [group_offsets(sizes, s) for s in stages]
 
 
-def kernel(sizes, local, dens_hbm, mom_hbm, fuel_hbm, modes_hbm, early_hbm, late_hbm,
+def kernel(sizes, local, dens_hbm, mom_hbm, fuel_hbm, modes_hbm, early_hbm, back_hbm, late_hbm,
            drate, mrate, hrate,
-           f, modes, early, late, edges, sides, ypack, zpack, ztile, stage_own, stage_got,
+           f, modes, early, back, late, edges, sides, ypack, zpack, ztile, stage_own, stage_got,
            load_sem, halo_send, halo_recv, stage_send, stage_recv):
     size_x, size_y, size_z = local
     rows = size_x * size_y
+    rows_z = 2 * ROWS
     me = {a: lax.axis_index(a) for a in sizes}
     stages = plan(sizes)
 
@@ -113,7 +140,7 @@
         pltpu.make_async_copy(src, dst, load_sem.at[i])
         for i, (src, dst) in enumerate([
             (dens_hbm, f.at[0, own]), (mom_hbm, f.at[1, own]), (early_hbm, early),
-            (fuel_hbm, f.at[2, own]), (modes_hbm, modes), (late_hbm, late),
+            (fuel_hbm, f.at[2, own]), (modes_hbm, modes), (late_hbm, late), (back_hbm, back),
         ])
     ]
     for copy in loads:
@@ -123,14 +150,14 @@
     for offset in partners:
         pl.semaphore_signal(barrier, inc=1, device_id=at(offset), device_id_type=MESH)
 
-    row = lax.broadcasted_iota(jnp.int32, (8, 2 * HALF), 0)
-    lane = lax.broadcasted_iota(jnp.int32, (8, 2 * HALF), 1)
+    row = lax.broadcasted_iota(jnp.int32, (ROWS, 2 * HALF), 0)
+    lane = lax.broadcasted_iota(jnp.int32, (ROWS, 2 * HALF), 1)
     pair = lax.rem(lane, HALF)
     kx = lax.div(pair, WIDTH)
     ky = pair - kx * WIDTH
-    turn = jnp.zeros((8, 2 * HALF), jnp.float32)
-    for k, axis, size in ((kx, "gx", size_x), (ky, "gy", size_y), (row, "gz", size_z)):
-        count = (k - KMAX).astype(jnp.float32) * me[axis].astype(jnp.float32)
+    turn = jnp.zeros((ROWS, 2 * HALF), jnp.float32)
+    for k, axis, size in ((kx - KMAX, "gx", size_x), (ky - KMAX, "gy", size_y), (row, "gz", size_z)):
+        count = k.astype(jnp.float32) * me[axis].astype(jnp.float32)
         part = count / sizes[axis]
         turn = turn + (part - jnp.floor(part))
     turn = turn - jnp.floor(turn + 0.5)
@@ -144,10 +171,12 @@
     loads[2].wait()
     flat = lambda i: f[i, own].reshape(rows, size_z)
     vel = flat(1) / flat(0)
-    trig_z = early[0:16]
-    trig_xy = early[24 : 24 + 2 * HALF]
-    grid = dot_nt(dot_nt(trig_z, vel), trig_xy)
-    cube = grid[0:8] + sign * pltpu.roll(grid[8:16], HALF, 1)
+    deep = 2 * rows_z
+    table_xy = early[deep : deep + 4 * HALF]
+    vel_both = jnp.concatenate(split(vel), 0)
+    part = fold(dot_split(early[0:deep], vel_both, ((1,), (1,))))
+    grid = fold(dot_split(jnp.concatenate(split(part), 0), table_xy, ((1,), (1,))))
+    cube = grid[0:ROWS] + sign * pltpu.roll(grid[ROWS:], HALF, 1)
     cube = cos_p * cube + sin_p * pltpu.roll(cube, HALF, 1)
     stage_own[0] = cube
 
@@ -181,6 +210,7 @@
         copy.start()
         return copy
 
+    loads[5].wait()
     halos_x = [
         send(f.at[:, pl.ds(size_x, REACH)], f.at[:, pl.ds(0, REACH)], 0, "gx", 1),
         send(f.at[:, pl.ds(REACH, REACH)], f.at[:, pl.ds(size_x + REACH, REACH)], 1, "gx", -1),
@@ -188,20 +218,22 @@
     for i in range(2):
         ypack[i, :, 0:REACH] = f[1 + i, own, 0:REACH]
         ypack[i, :, REACH : 2 * REACH] = f[1 + i, own, size_y - REACH : size_y]
-        zpack[i] = dot_nt(early[16:24], flat(1 + i))
+        zpack[i] = dot_nt(late[0:8], flat(1 + i))
     halos_y = [send(ypack, sides.at[0], 2, "gy", 1)]
     if sizes["gy"] > 2:
         halos_y.append(send(ypack, sides.at[1], 3, "gy", -1))
     halos_z = [send(zpack, ztile.at[0], 4, "gz", 1), send(zpack, ztile.at[1], 5, "gz", -1)]
 
     loads[4].wait()
-    hit_z = lax.broadcasted_iota(jnp.int32, (8, modes.shape[1]), 0) == modes[2:3] + KMAX
+    count = modes.shape[1]
+    row_z = lax.broadcasted_iota(jnp.int32, (ROWS, count), 0)
+    row_xy = lax.rem(lax.broadcasted_iota(jnp.int32, (2 * HALF, count), 0), HALF)
     code = (modes[0:1] + KMAX) * WIDTH + modes[1:2] + KMAX
-    hit_xy = lax.rem(lax.broadcasted_iota(jnp.int32, (2 * HALF, modes.shape[1]), 0), HALF) == code
-    chosen = dot_nt(hit_z.astype(jnp.float32), hit_xy.astype(jnp.float32))
-
-    loads[5].wait()
-    lap = [dot_nn(flat(1 + i), late[16 : 16 + size_z]).reshape(size_x, size_y, size_z) for i in range(2)]
+    hits = [((row_z == modes[2:3]), (row_xy == code)),
+            ((row_z == -modes[2:3]) & (row_z > 0), (row_xy == WIDTH * WIDTH - 1 - code))]
+    chosen = sum(dot_nt(hz.astype(jnp.float32), hxy.astype(jnp.float32)) for hz, hxy in hits)
+
+    lap = [dot_nn(flat(1 + i), late[24 : 24 + size_z]).reshape(size_x, size_y, size_z) for i in range(2)]
     outs = (drate, mrate, hrate)
     mrate[...] = lap[0]
     hrate[...] = lap[1]
@@ -220,7 +252,7 @@
         edges[i, :, 0:8] = sides[0, i]
         edges[i, :, 8 : 8 + size_y] = f[1 + i, own]
         edges[i, :, 8 + size_y : 16 + size_y] = sides[1 if sizes["gy"] > 2 else 0, i]
-        total = outs[1 + i][...] + dot_tn(tile, late[0:16]).reshape(size_x, size_y, size_z)
+        total = outs[1 + i][...] + dot_tn(tile, late[8:24]).reshape(size_x, size_y, size_z)
         for offset, weight in enumerate(SECOND_COEFFS, 1):
             total = total + weight * (
                 edges[i, :, 8 + offset : 8 + offset + size_y] + edges[i, :, 8 - offset : 8 - offset + size_y])
@@ -251,14 +283,20 @@
                   - mid_fuel * jnp.exp(-ACTIVATION * mid_fuel / planes(dens, 0)))
     mrate[...] = VISCOSITY * (mrate[...] + second_diff(mom)) - first_diff(mom * vel_pad + dens)
 
+    loads[6].wait()
     ncell = float(rows * size_z * math.prod(sizes.values()))
     cube = sum_stage(len(stages) - 1, pending)
-    coef = chosen * cube / ncell
-    energy = jnp.sum(jnp.sum(coef * coef, axis=1, keepdims=True), axis=0, keepdims=True)
+    coef = cube / ncell
+    picked = chosen * coef
+    energy = jnp.sum(jnp.sum(picked * coef, axis=1, keepdims=True), axis=0, keepdims=True)
     scale = 2.0 * FORCE_POWER / (energy + ENERGY_EPS)
-    local_coef = cos_p * coef - sin_p * pltpu.roll(coef, HALF, 1)
+    local_coef = cos_p * picked - sin_p * pltpu.roll(picked, HALF, 1)
     both = jnp.concatenate([local_coef, -sign * pltpu.roll(local_coef, HALF, 1)], 0)
-    low = dot_tn(dot_nn(both, trig_xy), trig_z).reshape(size_x, size_y, size_z)
+    wave = fold(dot_split(jnp.concatenate(split(both), 0), back[...], ((1,), (0,))))
+    high, rest = split(wave)
+    waves = jnp.concatenate([high, rest, high, rest], 0).T
+    low = dot_split(waves, early[deep + 4 * HALF : deep + 4 * HALF + 4 * rows_z], ((1,), (0,)))
+    low = low.reshape(size_x, size_y, size_z)
     mrate[...] = mrate[...] + f[0, own] * (low * scale.reshape(1, 1, 1))
     for copy in started + halos_x + halos_y + halos_z:
         copy.wait_send()
@@ -281,7 +319,7 @@
         size_x, size_y, size_z = local
         rows = size_x * size_y
         full = (size_x * sizes["gx"], size_y * sizes["gy"], size_z * sizes["gz"])
-        early, late = tables(local, full)
+        early, back, late = tables(local, full)
         modes = forced_modes.T
         stages = plan(sizes)
         messages = sum(len(g) for g in stages)
@@ -290,21 +328,22 @@
         rates = pl.pallas_call(
             functools.partial(kernel, sizes, local),
             out_shape=[pltpu.VMEM(local, f32)] * 3,
-            in_specs=[any_spec] * 6,
+            in_specs=[any_spec] * 7,
             out_specs=[pl.BlockSpec(memory_space=pltpu.VMEM)] * 3,
             scratch_shapes=[
                 pltpu.VMEM((3, size_x + 2 * REACH, size_y, size_z), f32),
                 pltpu.VMEM(modes.shape, jnp.int32),
-                pltpu.VMEM(early.shape, f32),
+                pltpu.VMEM(early.shape, jnp.bfloat16),
+                pltpu.VMEM(back.shape, jnp.bfloat16),
                 pltpu.VMEM(late.shape, f32),
                 pltpu.VMEM((2, size_x, size_y + 16, size_z), f32),
                 pltpu.VMEM((2, 2, size_x, 8, size_z), f32),
                 pltpu.VMEM((2, size_x, 8, size_z), f32),
                 pltpu.VMEM((2, 8, rows), f32),
                 pltpu.VMEM((2, 2, 8, rows), f32),
-                pltpu.VMEM((len(stages), 8, 2 * HALF), f32),
-                pltpu.VMEM((messages, 8, 2 * HALF), f32),
-                pltpu.SemaphoreType.DMA((6,)),
+                pltpu.VMEM((len(stages), ROWS, 2 * HALF), f32),
+                pltpu.VMEM((messages, ROWS, 2 * HALF), f32),
+                pltpu.SemaphoreType.DMA((7,)),
                 pltpu.SemaphoreType.DMA((6,)),
                 pltpu.SemaphoreType.DMA((6,)),
                 pltpu.SemaphoreType.DMA((messages,)),
@@ -312,7 +351,7 @@
             ],
             compiler_params=pltpu.CompilerParams(collective_id=0, has_side_effects=True),
             name="flame",
-        )(density, momentum, hydrogen, modes, jnp.asarray(early), jnp.asarray(late))
+        )(density, momentum, hydrogen, modes, jnp.asarray(early), jnp.asarray(back), jnp.asarray(late))
         return tuple(pl.pallas_call(
             write_out,
             out_shape=[jax.ShapeDtypeStruct(local, f32)] * 3,

time: 15 us -> 14.5 us (0.967)
  Pallas kernels: 14.2 us -> 13.7 us
    pallas_call x1, Pallas kernels: 13.5 us -> 13 us  [per_device(): pl.pallas_call(functools.partial(kernel, sizes, local), out_shape=[pltpu....]
where the time goes in v3:
time: 14.5 us; the launch traced here: 14.3 us
  Pallas kernels  13.7 us (94%)
  between operations  0.64 us (4%)
    pallas_call x1, Pallas kernels, per_device(): pl.pallas_call(functools.partial(kernel, sizes, local), out_shape=[pltpu....  13 us
    pallas_call x1, Pallas kernels, per_device(): pl.pallas_call(write_out, out_shape=[jax.ShapeDtypeStruct(local, f32)] *...  0.7 us

profile of v3, /device:TPU:0, one launch (start us, length us, event | category | flops | bytes accessed | tf_op | source)
XLA Modules:
  0.0 14.3 jit_solution(18415559233009166379)
XLA Ops:
  0.6 13.0 %flame.1 = (f32[8,16,128]{2,1,0:T(8,128)S(1)}, f32[8,16,128]{2,1,0:T(8,128)S(1)}, f32[8,16,128]{2,1,0:T(8,128)S(1)}) custom-call(f32[8,16,128]{2,1,0:T(8,128)} %dens_hbm.1, f32[8,16,128]{2,1,0:T(8,128)} %mom_hbm.1, f32[8,16,128]{2,1,0:T(8,128)} %fuel_hbm.1, s32[3,96]{1,0:T(4,128)} %bitcast.1, bf16[304,128]{1,0:T(8,128)(2,1)} %constant.6.clone.early_hbm, ...), custom_call_target="tpu_custom_call" | custom-call | tf_op jit(solution)/shard_map/flame/pallas_call | solution.py:328
  13.6 0.7 %write.1 = (f32[8,16,128]{2,1,0:T(8,128)}, f32[8,16,128]{2,1,0:T(8,128)}, f32[8,16,128]{2,1,0:T(8,128)}) custom-call(f32[8,16,128]{2,1,0:T(8,128)S(1)} %get-tuple-element.6.refs_0_, f32[8,16,128]{2,1,0:T(8,128)S(1)} %get-tuple-element.7.refs_1_, f32[8,16,128]{2,1,0:T(8,128)S(1)} %get-tuple-element.8.refs_2_), custom_call_target="tpu_custom_call" | custom-call | tf_op jit(solution)/shard_map/write/pallas_call | solution.py:355

commit v4 on v3

--- a/solution.py
+++ b/solution.py
@@ -115,11 +115,13 @@
 
 
 def plan(sizes):
-    if sizes["gx"] * sizes["gy"] <= 16:
+    if math.prod(sizes.values()) <= 32:
+        stages = [("gz", "gy", "gx")]
+    elif sizes["gx"] * sizes["gy"] <= 16:
         stages = [("gz",), ("gx", "gy")]
     else:
         stages = [("gz",), ("gx",), ("gy",)]
-    return [group_offsets(sizes, s) for s in stages]
+    return [group_offsets(sizes, s)[::-1] for s in stages]
 
 
 def kernel(sizes, local, dens_hbm, mom_hbm, fuel_hbm, modes_hbm, early_hbm, back_hbm, late_hbm,

time: 14.5 us -> 14.4 us (level)
  no operation moved by 1% of the time
where the time goes in v4:
time: 14.4 us; the launch traced here: 14.2 us
  Pallas kernels  13.6 us (94%)
  between operations  0.64 us (4%)
    pallas_call x1, Pallas kernels, per_device(): pl.pallas_call(functools.partial(kernel, sizes, local), out_shape=[pltpu....  12.9 us
    pallas_call x1, Pallas kernels, per_device(): pl.pallas_call(write_out, out_shape=[jax.ShapeDtypeStruct(local, f32)] *...  0.7 us

profile of v4, /device:TPU:0, one launch (start us, length us, event | category | flops | bytes accessed | tf_op | source)
XLA Modules:
  0.0 14.2 jit_solution(16047062022767808483)
XLA Ops:
  0.6 12.9 %flame.1 = (f32[8,16,128]{2,1,0:T(8,128)S(1)}, f32[8,16,128]{2,1,0:T(8,128)S(1)}, f32[8,16,128]{2,1,0:T(8,128)S(1)}) custom-call(f32[8,16,128]{2,1,0:T(8,128)} %dens_hbm.1, f32[8,16,128]{2,1,0:T(8,128)} %mom_hbm.1, f32[8,16,128]{2,1,0:T(8,128)} %fuel_hbm.1, s32[3,96]{1,0:T(4,128)} %bitcast.1, bf16[304,128]{1,0:T(8,128)(2,1)} %constant.6.clone.early_hbm, ...), custom_call_target="tpu_custom_call" | custom-call | tf_op jit(solution)/shard_map/flame/pallas_call | solution.py:330
  13.5 0.7 %write.1 = (f32[8,16,128]{2,1,0:T(8,128)}, f32[8,16,128]{2,1,0:T(8,128)}, f32[8,16,128]{2,1,0:T(8,128)}) custom-call(f32[8,16,128]{2,1,0:T(8,128)S(1)} %get-tuple-element.6.refs_0_, f32[8,16,128]{2,1,0:T(8,128)S(1)} %get-tuple-element.7.refs_1_, f32[8,16,128]{2,1,0:T(8,128)S(1)} %get-tuple-element.8.refs_2_), custom_call_target="tpu_custom_call" | custom-call | tf_op jit(solution)/shard_map/write/pallas_call | solution.py:357

commit v5 on v4

--- a/solution.py
+++ b/solution.py
@@ -182,27 +182,29 @@
     cube = cos_p * cube + sin_p * pltpu.roll(cube, HALF, 1)
     stage_own[0] = cube
 
+    def span(s):
+        base = sum(len(g) for g in stages[:s])
+        return pl.ds(base, len(stages[s]))
+
     def send_stage(s):
         base = sum(len(g) for g in stages[:s])
-        copies = []
         for i, offset in enumerate(stages[s]):
-            copy = pltpu.make_async_remote_copy(
+            pltpu.make_async_remote_copy(
                 src_ref=stage_own.at[s], dst_ref=stage_got.at[base + i],
-                send_sem=stage_send.at[base + i], recv_sem=stage_recv.at[base + i],
-                device_id=at(offset), device_id_type=MESH)
-            copy.start()
-            copies.append(copy)
-        return copies
-
-    def sum_stage(s, copies):
+                send_sem=stage_send.at[s], recv_sem=stage_recv.at[s],
+                device_id=at(offset), device_id_type=MESH).start()
+
+    def wait_stage(s, sem):
+        got = stage_got.at[span(s)]
+        pltpu.make_async_copy(got, got, sem.at[s]).wait()
+
+    def sum_stage(s):
         base = sum(len(g) for g in stages[:s])
-        for copy in copies:
-            copy.wait_recv()
-        return tree_sum([stage_own[s]] + [stage_got[base + i] for i in range(len(copies))])
+        wait_stage(s, stage_recv)
+        return tree_sum([stage_own[s]] + [stage_got[base + i] for i in range(len(stages[s]))])
 
     pl.semaphore_wait(barrier, len(partners))
-    pending = send_stage(0)
-    started = list(pending)
+    send_stage(0)
     loads[3].wait()
 
     def send(src, dst, slot, axis, step):
@@ -241,9 +243,8 @@
     hrate[...] = lap[1]
 
     for s in range(1, len(stages)):
-        stage_own[s] = sum_stage(s - 1, pending)
-        pending = send_stage(s)
-        started += pending
+        stage_own[s] = sum_stage(s - 1)
+        send_stage(s)
 
     for copy in halos_z:
         copy.wait_recv()
@@ -287,7 +288,7 @@
 
     loads[6].wait()
     ncell = float(rows * size_z * math.prod(sizes.values()))
-    cube = sum_stage(len(stages) - 1, pending)
+    cube = sum_stage(len(stages) - 1)
     coef = cube / ncell
     picked = chosen * coef
     energy = jnp.sum(jnp.sum(picked * coef, axis=1, keepdims=True), axis=0, keepdims=True)
@@ -300,8 +301,10 @@
     low = dot_split(waves, early[deep + 4 * HALF : deep + 4 * HALF + 4 * rows_z], ((1,), (0,)))
     low = low.reshape(size_x, size_y, size_z)
     mrate[...] = mrate[...] + f[0, own] * (low * scale.reshape(1, 1, 1))
-    for copy in started + halos_x + halos_y + halos_z:
+    for copy in halos_x + halos_y + halos_z:
         copy.wait_send()
+    for s in range(len(stages)):
+        wait_stage(s, stage_send)
 
 
 def write_out(*refs):
@@ -348,8 +351,8 @@
                 pltpu.SemaphoreType.DMA((7,)),
                 pltpu.SemaphoreType.DMA((6,)),
                 pltpu.SemaphoreType.DMA((6,)),
-                pltpu.SemaphoreType.DMA((messages,)),
-                pltpu.SemaphoreType.DMA((messages,)),
+                pltpu.SemaphoreType.DMA((len(stages),)),
+                pltpu.SemaphoreType.DMA((len(stages),)),
             ],
             compiler_params=pltpu.CompilerParams(collective_id=0, has_side_effects=True),
             name="flame",

time: 14.4 us -> 13.7 us (0.951)
  Pallas kernels: 13.6 us -> 12.9 us
    pallas_call x1, Pallas kernels: 12.9 us -> 12.2 us  [per_device(): pl.pallas_call(functools.partial(kernel, sizes, local), out_shape=[pltpu....]
where the time goes in v5:
time: 13.7 us; the launch traced here: 13.6 us
  Pallas kernels  12.9 us (94%)
  between operations  0.64 us (5%)
    pallas_call x1, Pallas kernels, per_device(): pl.pallas_call(functools.partial(kernel, sizes, local), out_shape=[pltpu....  12.2 us
    pallas_call x1, Pallas kernels, per_device(): pl.pallas_call(write_out, out_shape=[jax.ShapeDtypeStruct(local, f32)] *...  0.7 us

profile of v5, /device:TPU:0, one launch (start us, length us, event | category | flops | bytes accessed | tf_op | source)
XLA Modules:
  0.0 13.6 jit_solution(435087844563908339)
XLA Ops:
  0.6 12.2 %flame.1 = (f32[8,16,128]{2,1,0:T(8,128)S(1)}, f32[8,16,128]{2,1,0:T(8,128)S(1)}, f32[8,16,128]{2,1,0:T(8,128)S(1)}) custom-call(f32[8,16,128]{2,1,0:T(8,128)} %dens_hbm.1, f32[8,16,128]{2,1,0:T(8,128)} %mom_hbm.1, f32[8,16,128]{2,1,0:T(8,128)} %fuel_hbm.1, s32[3,96]{1,0:T(4,128)} %bitcast.1, bf16[304,128]{1,0:T(8,128)(2,1)} %constant.6.clone.early_hbm, ...), custom_call_target="tpu_custom_call" | custom-call | tf_op jit(solution)/shard_map/flame/pallas_call | solution.py:333
  12.9 0.7 %write.1 = (f32[8,16,128]{2,1,0:T(8,128)}, f32[8,16,128]{2,1,0:T(8,128)}, f32[8,16,128]{2,1,0:T(8,128)}) custom-call(f32[8,16,128]{2,1,0:T(8,128)S(1)} %get-tuple-element.6.refs_0_, f32[8,16,128]{2,1,0:T(8,128)S(1)} %get-tuple-element.7.refs_1_, f32[8,16,128]{2,1,0:T(8,128)S(1)} %get-tuple-element.8.refs_2_), custom_call_target="tpu_custom_call" | custom-call | tf_op jit(solution)/shard_map/write/pallas_call | solution.py:360

commit v6 on v5

--- a/solution.py
+++ b/solution.py
@@ -60,9 +60,10 @@
                     halo[8 + q - size_z, z] = weight
     z_high, z_low = split_host(trig_z)
     xy_high, xy_low = split_host(trig_xy)
-    early = np.concatenate([z_high, z_low, xy_high, xy_low, z_high, z_high, z_low, z_low], 0)
+    early = np.concatenate([z_high, z_low, xy_high, xy_low, z_high, z_high, z_low, z_low,
+                            split_host(np.concatenate([edge, np.zeros_like(edge)], 0))[0]], 0)
     back = np.concatenate([xy_high, xy_low], 1)
-    late = np.concatenate([edge, halo, band], 0).astype(np.float32)
+    late = np.concatenate([halo, band], 0).astype(np.float32)
     return early, back, late
 
 
@@ -203,9 +204,20 @@
         wait_stage(s, stage_recv)
         return tree_sum([stage_own[s]] + [stage_got[base + i] for i in range(len(stages[s]))])
 
+    loads[3].wait()
+    pieces = []
+    for i in range(2):
+        ypack[i, :, 0:REACH] = f[1 + i, own, 0:REACH]
+        ypack[i, :, REACH : 2 * REACH] = f[1 + i, own, size_y - REACH : size_y]
+        high, rest = split(flat(1 + i))
+        pieces += [high, *split(rest)]
+    edge_at = deep + 4 * HALF + 4 * rows_z
+    ends = dot_split(early[edge_at : edge_at + 16], jnp.concatenate(pieces, 0), ((1,), (1,)))[0:8]
+    for i in range(2):
+        zpack[i] = tree_sum([ends[:, (3 * i + j) * rows : (3 * i + j + 1) * rows] for j in range(3)])
+
     pl.semaphore_wait(barrier, len(partners))
     send_stage(0)
-    loads[3].wait()
 
     def send(src, dst, slot, axis, step):
         copy = pltpu.make_async_remote_copy(
@@ -214,15 +226,10 @@
         copy.start()
         return copy
 
-    loads[5].wait()
     halos_x = [
         send(f.at[:, pl.ds(size_x, REACH)], f.at[:, pl.ds(0, REACH)], 0, "gx", 1),
         send(f.at[:, pl.ds(REACH, REACH)], f.at[:, pl.ds(size_x + REACH, REACH)], 1, "gx", -1),
     ]
-    for i in range(2):
-        ypack[i, :, 0:REACH] = f[1 + i, own, 0:REACH]
-        ypack[i, :, REACH : 2 * REACH] = f[1 + i, own, size_y - REACH : size_y]
-        zpack[i] = dot_nt(late[0:8], flat(1 + i))
     halos_y = [send(ypack, sides.at[0], 2, "gy", 1)]
     if sizes["gy"] > 2:
         halos_y.append(send(ypack, sides.at[1], 3, "gy", -1))
@@ -237,7 +244,8 @@
             ((row_z == -modes[2:3]) & (row_z > 0), (row_xy == WIDTH * WIDTH - 1 - code))]
     chosen = sum(dot_nt(hz.astype(jnp.float32), hxy.astype(jnp.float32)) for hz, hxy in hits)
 
-    lap = [dot_nn(flat(1 + i), late[24 : 24 + size_z]).reshape(size_x, size_y, size_z) for i in range(2)]
+    loads[5].wait()
+    lap = [dot_nn(flat(1 + i), late[16 : 16 + size_z]).reshape(size_x, size_y, size_z) for i in range(2)]
     outs = (drate, mrate, hrate)
     mrate[...] = lap[0]
     hrate[...] = lap[1]
@@ -255,7 +263,7 @@
         edges[i, :, 0:8] = sides[0, i]
         edges[i, :, 8 : 8 + size_y] = f[1 + i, own]
         edges[i, :, 8 + size_y : 16 + size_y] = sides[1 if sizes["gy"] > 2 else 0, i]
-        total = outs[1 + i][...] + dot_tn(tile, late[8:24]).reshape(size_x, size_y, size_z)
+        total = outs[1 + i][...] + dot_tn(tile, late[0:16]).reshape(size_x, size_y, size_z)
         for offset, weight in enumerate(SECOND_COEFFS, 1):
             total = total + weight * (
                 edges[i, :, 8 + offset : 8 + offset + size_y] + edges[i, :, 8 - offset : 8 - offset + size_y])

time: 13.7 us -> 13.5 us (0.985)
  Pallas kernels: 12.9 us -> 12.7 us
    pallas_call x1, Pallas kernels: 12.2 us -> 12 us  [per_device(): pl.pallas_call(functools.partial(kernel, sizes, local), out_shape=[pltpu....]
where the time goes in v6:
time: 13.5 us; the launch traced here: 13.4 us
  Pallas kernels  12.7 us (94%)
  between operations  0.64 us (5%)
    pallas_call x1, Pallas kernels, per_device(): pl.pallas_call(functools.partial(kernel, sizes, local), out_shape=[pltpu....  12 us
    pallas_call x1, Pallas kernels, per_device(): pl.pallas_call(write_out, out_shape=[jax.ShapeDtypeStruct(local, f32)] *...  0.7 us

profile of v6, /device:TPU:0, one launch (start us, length us, event | category | flops | bytes accessed | tf_op | source)
XLA Modules:
  0.0 13.4 jit_solution(3567191959568230598)
XLA Ops:
  0.6 12.0 %flame.1 = (f32[8,16,128]{2,1,0:T(8,128)S(1)}, f32[8,16,128]{2,1,0:T(8,128)S(1)}, f32[8,16,128]{2,1,0:T(8,128)S(1)}) custom-call(f32[8,16,128]{2,1,0:T(8,128)} %dens_hbm.1, f32[8,16,128]{2,1,0:T(8,128)} %mom_hbm.1, f32[8,16,128]{2,1,0:T(8,128)} %fuel_hbm.1, s32[3,96]{1,0:T(4,128)} %bitcast.1, bf16[320,128]{1,0:T(8,128)(2,1)} %constant.6.clone.early_hbm, ...), custom_call_target="tpu_custom_call" | custom-call | tf_op jit(solution)/shard_map/flame/pallas_call | solution.py:341
  12.7 0.7 %write.1 = (f32[8,16,128]{2,1,0:T(8,128)}, f32[8,16,128]{2,1,0:T(8,128)}, f32[8,16,128]{2,1,0:T(8,128)}) custom-call(f32[8,16,128]{2,1,0:T(8,128)S(1)} %get-tuple-element.6.refs_0_, f32[8,16,128]{2,1,0:T(8,128)S(1)} %get-tuple-element.7.refs_1_, f32[8,16,128]{2,1,0:T(8,128)S(1)} %get-tuple-element.8.refs_2_), custom_call_target="tpu_custom_call" | custom-call | tf_op jit(solution)/shard_map/write/pallas_call | solution.py:368

commit v7 on v6

--- a/solution.py
+++ b/solution.py
@@ -27,6 +27,28 @@
 MESH = pl.DeviceIdType.MESH
 
 
+def packed_modes():
+    reach = range(-KMAX, KMAX + 1)
+    cells = [(x, y, z) for z in range(ROWS) for x in reach for y in reach
+             if x * x + y * y + z * z <= KMAX * KMAX and (z, x, y) > (0, 0, 0)]
+    return cells
+
+
+def packed_index(place):
+    cells = packed_modes()
+    result = []
+    for part in range(3):
+        value = jnp.full(place.shape, cells[0][part], jnp.int32)
+        if part == 1:
+            value = value + place
+        for i in range(1, len(cells)):
+            step = cells[i][part] - cells[i - 1][part] - (part == 1)
+            if step:
+                value = value + jnp.where(place >= i, step, 0)
+        result.append(value)
+    return result
+
+
 def tables(local, full):
     size_x, size_y, size_z = local
     full_x, full_y, full_z = full
@@ -37,11 +59,11 @@
     trig_z[ROWS:] = np.sin(ang_z[KMAX:])
     ax = k[:, None] * np.arange(size_x)[None, :] / full_x
     ay = k[:, None] * np.arange(size_y)[None, :] / full_y
-    ang = 2.0 * np.pi * (ax[:, None, :, None] + ay[None, :, None, :])
-    ang = ang.reshape(WIDTH * WIDTH, size_x * size_y)
+    ang = np.stack([2.0 * np.pi * (ax[x + KMAX, :, None] + ay[y + KMAX, None, :]) for x, y, _ in packed_modes()])
+    ang = ang.reshape(-1, size_x * size_y)
     trig_xy = np.zeros((2 * HALF, size_x * size_y))
-    trig_xy[: WIDTH * WIDTH] = np.cos(ang)
-    trig_xy[HALF : HALF + WIDTH * WIDTH] = np.sin(ang)
+    trig_xy[: len(ang)] = np.cos(ang)
+    trig_xy[HALF : HALF + len(ang)] = np.sin(ang)
     edge = np.zeros((8, size_z))
     for j in range(REACH):
         edge[j, j] = 1.0
@@ -153,16 +175,13 @@
     for offset in partners:
         pl.semaphore_signal(barrier, inc=1, device_id=at(offset), device_id_type=MESH)
 
-    row = lax.broadcasted_iota(jnp.int32, (ROWS, 2 * HALF), 0)
-    lane = lax.broadcasted_iota(jnp.int32, (ROWS, 2 * HALF), 1)
-    pair = lax.rem(lane, HALF)
-    kx = lax.div(pair, WIDTH)
-    ky = pair - kx * WIDTH
-    turn = jnp.zeros((ROWS, 2 * HALF), jnp.float32)
-    for k, axis, size in ((kx - KMAX, "gx", size_x), (ky - KMAX, "gy", size_y), (row, "gz", size_z)):
-        count = k.astype(jnp.float32) * me[axis].astype(jnp.float32)
-        part = count / sizes[axis]
+    lane = lax.broadcasted_iota(jnp.int32, (1, 2 * HALF), 1)
+    kx, ky, kz = packed_index(lax.rem(lane, HALF))
+    turn = jnp.zeros((1, 2 * HALF), jnp.float32)
+    for k, axis in ((kx, "gx"), (ky, "gy"), (kz, "gz")):
+        part = k.astype(jnp.float32) * me[axis].astype(jnp.float32) / sizes[axis]
         turn = turn + (part - jnp.floor(part))
+    level = (lax.broadcasted_iota(jnp.int32, (ROWS, 2 * HALF), 0) == kz).astype(jnp.float32)
     turn = turn - jnp.floor(turn + 0.5)
     cos_p = jnp.cos(2.0 * math.pi * turn)
     sin_p = jnp.sin(2.0 * math.pi * turn)
@@ -179,7 +198,9 @@
     vel_both = jnp.concatenate(split(vel), 0)
     part = fold(dot_split(early[0:deep], vel_both, ((1,), (1,))))
     grid = fold(dot_split(jnp.concatenate(split(part), 0), table_xy, ((1,), (1,))))
-    cube = grid[0:ROWS] + sign * pltpu.roll(grid[ROWS:], HALF, 1)
+    grid = grid * jnp.concatenate([level, level], 0)
+    flip = jnp.sum(grid[ROWS:], axis=0, keepdims=True)
+    cube = jnp.sum(grid[0:ROWS], axis=0, keepdims=True) + sign * pltpu.roll(flip, HALF, 1)
     cube = cos_p * cube + sin_p * pltpu.roll(cube, HALF, 1)
     stage_own[0] = cube
 
@@ -237,12 +258,13 @@
 
     loads[4].wait()
     count = modes.shape[1]
-    row_z = lax.broadcasted_iota(jnp.int32, (ROWS, count), 0)
-    row_xy = lax.rem(lax.broadcasted_iota(jnp.int32, (2 * HALF, count), 0), HALF)
-    code = (modes[0:1] + KMAX) * WIDTH + modes[1:2] + KMAX
-    hits = [((row_z == modes[2:3]), (row_xy == code)),
-            ((row_z == -modes[2:3]) & (row_z > 0), (row_xy == WIDTH * WIDTH - 1 - code))]
-    chosen = sum(dot_nt(hz.astype(jnp.float32), hxy.astype(jnp.float32)) for hz, hxy in hits)
+    code = (modes[0:1] * WIDTH + modes[1:2]) * WIDTH + modes[2:3]
+    place = lax.rem(lax.broadcasted_iota(jnp.int32, (2 * HALF, 1), 0), HALF)
+    px, py, pz = packed_index(place)
+    mine = (px * WIDTH + py) * WIDTH + pz
+    used = place < len(packed_modes())
+    both_ways = jnp.where(used & (mine == code), 1.0, 0.0) + jnp.where(used & (mine == -code), 1.0, 0.0)
+    chosen = dot_nt(jnp.ones((8, count), jnp.float32), both_ways)[0:1]
 
     loads[5].wait()
     lap = [dot_nn(flat(1 + i), late[16 : 16 + size_z]).reshape(size_x, size_y, size_z) for i in range(2)]
@@ -302,7 +324,7 @@
     energy = jnp.sum(jnp.sum(picked * coef, axis=1, keepdims=True), axis=0, keepdims=True)
     scale = 2.0 * FORCE_POWER / (energy + ENERGY_EPS)
     local_coef = cos_p * picked - sin_p * pltpu.roll(picked, HALF, 1)
-    both = jnp.concatenate([local_coef, -sign * pltpu.roll(local_coef, HALF, 1)], 0)
+    both = jnp.concatenate([level * local_coef, level * (-sign * pltpu.roll(local_coef, HALF, 1))], 0)
     wave = fold(dot_split(jnp.concatenate(split(both), 0), back[...], ((1,), (0,))))
     high, rest = split(wave)
     waves = jnp.concatenate([high, rest, high, rest], 0).T
@@ -354,8 +376,8 @@
                 pltpu.VMEM((2, size_x, 8, size_z), f32),
                 pltpu.VMEM((2, 8, rows), f32),
                 pltpu.VMEM((2, 2, 8, rows), f32),
-                pltpu.VMEM((len(stages), ROWS, 2 * HALF), f32),
-                pltpu.VMEM((messages, ROWS, 2 * HALF), f32),
+                pltpu.VMEM((len(stages), 1, 2 * HALF), f32),
+                pltpu.VMEM((messages, 1, 2 * HALF), f32),
                 pltpu.SemaphoreType.DMA((7,)),
                 pltpu.SemaphoreType.DMA((6,)),
                 pltpu.SemaphoreType.DMA((6,)),

time: 13.5 us -> 13.1 us (0.970)
  Pallas kernels: 12.7 us -> 12.3 us
    pallas_call x1, Pallas kernels: 12 us -> 11.6 us  [per_device(): pl.pallas_call(functools.partial(kernel, sizes, local), out_shape=[pltpu....]
where the time goes in v7:
time: 13.1 us; the launch traced here: 12.9 us
  Pallas kernels  12.3 us (94%)
  between operations  0.64 us (5%)
    pallas_call x1, Pallas kernels, per_device(): pl.pallas_call(functools.partial(kernel, sizes, local), out_shape=[pltpu....  11.6 us
    pallas_call x1, Pallas kernels, per_device(): pl.pallas_call(write_out, out_shape=[jax.ShapeDtypeStruct(local, f32)] *...  0.7 us

profile of v7, /device:TPU:0, one launch (start us, length us, event | category | flops | bytes accessed | tf_op | source)
XLA Modules:
  0.0 12.9 jit_solution(12622786217651789238)
XLA Ops:
  0.6 11.6 %flame.1 = (f32[8,16,128]{2,1,0:T(8,128)S(1)}, f32[8,16,128]{2,1,0:T(8,128)S(1)}, f32[8,16,128]{2,1,0:T(8,128)S(1)}) custom-call(f32[8,16,128]{2,1,0:T(8,128)} %dens_hbm.1, f32[8,16,128]{2,1,0:T(8,128)} %mom_hbm.1, f32[8,16,128]{2,1,0:T(8,128)} %fuel_hbm.1, s32[3,96]{1,0:T(4,128)} %bitcast.1, bf16[320,128]{1,0:T(8,128)(2,1)} %constant.6.clone.early_hbm, ...), custom_call_target="tpu_custom_call" | custom-call | tf_op jit(solution)/shard_map/flame/pallas_call | solution.py:363
  12.2 0.7 %write.1 = (f32[8,16,128]{2,1,0:T(8,128)}, f32[8,16,128]{2,1,0:T(8,128)}, f32[8,16,128]{2,1,0:T(8,128)}) custom-call(f32[8,16,128]{2,1,0:T(8,128)S(1)} %get-tuple-element.6.refs_0_, f32[8,16,128]{2,1,0:T(8,128)S(1)} %get-tuple-element.7.refs_1_, f32[8,16,128]{2,1,0:T(8,128)S(1)} %get-tuple-element.8.refs_2_), custom_call_target="tpu_custom_call" | custom-call | tf_op jit(solution)/shard_map/write/pallas_call | solution.py:390

commit v8 on v7

--- a/solution.py
+++ b/solution.py
@@ -242,7 +242,7 @@
 
     def send(src, dst, slot, axis, step):
         copy = pltpu.make_async_remote_copy(
-            src_ref=src, dst_ref=dst, send_sem=halo_send.at[slot], recv_sem=halo_recv.at[slot],
+            src_ref=src, dst_ref=dst, send_sem=halo_send.at[slot // 2], recv_sem=halo_recv.at[slot // 2],
             device_id=at({axis: step % sizes[axis]}), device_id_type=MESH)
         copy.start()
         return copy
@@ -276,10 +276,12 @@
         stage_own[s] = sum_stage(s - 1)
         send_stage(s)
 
-    for copy in halos_z:
-        copy.wait_recv()
-    for copy in halos_y:
-        copy.wait_recv()
+    arrived = [f.at[:, pl.ds(0, 2 * REACH)], sides.at[pl.ds(0, len(halos_y))], ztile]
+    def wait_halo(sem, slot):
+        pltpu.make_async_copy(arrived[slot], arrived[slot], sem.at[slot]).wait()
+
+    wait_halo(halo_recv, 2)
+    wait_halo(halo_recv, 1)
     for i in range(2):
         tile = jnp.concatenate([ztile[0, i], ztile[1, i]], 0)
         edges[i, :, 0:8] = sides[0, i]
@@ -291,8 +293,7 @@
                 edges[i, :, 8 + offset : 8 + offset + size_y] + edges[i, :, 8 - offset : 8 - offset + size_y])
         outs[1 + i][...] = total
 
-    for copy in halos_x:
-        copy.wait_recv()
+    wait_halo(halo_recv, 0)
     def planes(x, offset):
         return x[REACH + offset : REACH + offset + size_x]
 
@@ -331,8 +332,8 @@
     low = dot_split(waves, early[deep + 4 * HALF : deep + 4 * HALF + 4 * rows_z], ((1,), (0,)))
     low = low.reshape(size_x, size_y, size_z)
     mrate[...] = mrate[...] + f[0, own] * (low * scale.reshape(1, 1, 1))
-    for copy in halos_x + halos_y + halos_z:
-        copy.wait_send()
+    for slot in range(3):
+        wait_halo(halo_send, slot)
     for s in range(len(stages)):
         wait_stage(s, stage_send)
 
@@ -379,8 +380,8 @@
                 pltpu.VMEM((len(stages), 1, 2 * HALF), f32),
                 pltpu.VMEM((messages, 1, 2 * HALF), f32),
                 pltpu.SemaphoreType.DMA((7,)),
-                pltpu.SemaphoreType.DMA((6,)),
-                pltpu.SemaphoreType.DMA((6,)),
+                pltpu.SemaphoreType.DMA((3,)),
+                pltpu.SemaphoreType.DMA((3,)),
                 pltpu.SemaphoreType.DMA((len(stages),)),
                 pltpu.SemaphoreType.DMA((len(stages),)),
             ],

time: 13.1 us -> 13 us (level)
  no operation moved by 1% of the time
where the time goes in v8:
time: 13 us; the launch traced here: 12.9 us
  Pallas kernels  12.2 us (94%)
  between operations  0.64 us (5%)
    pallas_call x1, Pallas kernels, per_device(): pl.pallas_call(functools.partial(kernel, sizes, local), out_shape=[pltpu....  11.5 us
    pallas_call x1, Pallas kernels, per_device(): pl.pallas_call(write_out, out_shape=[jax.ShapeDtypeStruct(local, f32)] *...  0.7 us

profile of v8, /device:TPU:0, one launch (start us, length us, event | category | flops | bytes accessed | tf_op | source)
XLA Modules:
  0.0 12.9 jit_solution(17999854035865758852)
XLA Ops:
  0.6 11.5 %flame.1 = (f32[8,16,128]{2,1,0:T(8,128)S(1)}, f32[8,16,128]{2,1,0:T(8,128)S(1)}, f32[8,16,128]{2,1,0:T(8,128)S(1)}) custom-call(f32[8,16,128]{2,1,0:T(8,128)} %dens_hbm.1, f32[8,16,128]{2,1,0:T(8,128)} %mom_hbm.1, f32[8,16,128]{2,1,0:T(8,128)} %fuel_hbm.1, s32[3,96]{1,0:T(4,128)} %bitcast.1, bf16[320,128]{1,0:T(8,128)(2,1)} %constant.6.clone.early_hbm, ...), custom_call_target="tpu_custom_call" | custom-call | tf_op jit(solution)/shard_map/flame/pallas_call | solution.py:364
  12.2 0.7 %write.1 = (f32[8,16,128]{2,1,0:T(8,128)}, f32[8,16,128]{2,1,0:T(8,128)}, f32[8,16,128]{2,1,0:T(8,128)}) custom-call(f32[8,16,128]{2,1,0:T(8,128)S(1)} %get-tuple-element.6.refs_0_, f32[8,16,128]{2,1,0:T(8,128)S(1)} %get-tuple-element.7.refs_1_, f32[8,16,128]{2,1,0:T(8,128)S(1)} %get-tuple-element.8.refs_2_), custom_call_target="tpu_custom_call" | custom-call | tf_op jit(solution)/shard_map/write/pallas_call | solution.py:391
